TPU v7x, 32 devices: a whole 2x2x4 slice. The times are simulated.
32 devices in a mesh: dp: 2 (over x), expert: 4 (over z), tensor: 4 (over y, core).
Axes of the slice: x: 2, y: 2, z: 4, core: 2. Of those that a mesh axis runs over, the one named last changes fastest.
Arguments:
- tokens: bfloat16 [1024, 7168], P(('dp', 'expert'), 'tensor'), may hold values from -6 to 6
- expert_ids: int32 [1024, 2], P(('dp', 'expert')), may hold values from 0 to 3, all different within a row; in each aligned block of 128 rows (0 to 127, 128 to 255, ...) at most 96 rows name the same one
- gate_scores: bfloat16 [1024, 2], P(('dp', 'expert')), may hold values from 0.099609375 to 0.59765625
- weight_in: bfloat16 [4, 2, 7168, 1024], P('expert', None, 'tensor', 'dp'), may hold values from -0.0625 to 0.0625
- weight_out: bfloat16 [4, 1024, 7168], P('expert', 'dp', 'tensor'), may hold values from -0.1875 to 0.1875
Outputs:
- mixed: bfloat16 [1024, 7168], P(('dp', 'expert'), 'tensor')
Inputs may be any that keep to these rules, and one draw needn't show every extreme that they name: `expert_ids`: each token names 2 different experts; among the 128 tokens of one index of dp and expert together (aligned blocks of rows) no expert is named more than 96 times, and in some blocks an expert is named exactly 96 times.
All inputs are finite; a program needn't handle non-finite values.
Results may differ from a plain program's by a relative error of at most 0.0071.
Values may be sent and summed in bfloat16 or wider, within the bound.
A program may use at most 64 MiB of HBM per device.

v0:
```python
import jax
import jax.numpy as jnp
from jax import lax
from jax.sharding import PartitionSpec as P


def per_device(tokens, expert_ids, gate_scores, weight_in, weight_out):
    experts = lax.axis_size("expert")
    tok_count, top_count = expert_ids.shape
    capacity = min(3 * tok_count * top_count // (2 * experts), tok_count)
    width_all = tokens.shape[1] * lax.axis_size("tensor")
    wide = tokens.astype(jnp.float32)
    row_squares = lax.psum(jnp.sum(wide * wide, axis=1, keepdims=True), "tensor")
    normed = (wide * lax.rsqrt(row_squares / width_all + 1e-06)).astype(jnp.bfloat16)
    flat_ids = expert_ids.reshape(-1)
    one_hot = (flat_ids[:, None] == jnp.arange(experts, dtype=jnp.int32)[None, :]).astype(jnp.int32)
    earlier = jnp.cumsum(one_hot, axis=0) - one_hot
    slot_pos = jnp.sum(earlier * one_hot, axis=1)
    target = flat_ids * capacity + slot_pos
    chosen = (target[:, None] == jnp.arange(experts * capacity, dtype=jnp.int32)[None, :]).astype(
        jnp.float32
    )
    chosen = chosen.reshape(tok_count, top_count, experts * capacity)
    picked = jnp.sum(chosen, axis=1).astype(jnp.bfloat16)
    combine_weight = jnp.sum(chosen * gate_scores.astype(jnp.float32)[:, :, None], axis=1).astype(
        jnp.bfloat16
    )
    outgoing = jnp.einsum("ts,td->sd", picked, normed, preferred_element_type=jnp.float32).astype(
        jnp.bfloat16
    )
    outgoing = outgoing.reshape(experts, capacity, tokens.shape[1])
    arrived = lax.all_to_all(outgoing, "expert", split_axis=0, concat_axis=0, tiled=True)
    slot_rows = arrived.reshape(experts * capacity, tokens.shape[1])
    local_in = weight_in[0]
    partial_sums = jnp.einsum(
        "rd,gdf->rgf",
        lax.all_gather(slot_rows, "dp", axis=0, tiled=True),
        local_in,
        preferred_element_type=jnp.float32,
    )
    summed = lax.psum_scatter(partial_sums, "tensor", scatter_dimension=2, tiled=True)
    hidden = (jax.nn.silu(summed[:, 0]) * summed[:, 1]).astype(jnp.bfloat16)
    hidden = lax.all_to_all(hidden[:, None, :], "dp", split_axis=0, concat_axis=1, tiled=True)
    row_count = hidden.shape[0]
    hidden_full = lax.all_gather(hidden, "tensor", axis=2, tiled=True).reshape(row_count, -1)
    expert_out = jnp.dot(
        hidden_full,
        lax.all_gather(weight_out[0], "dp", axis=0, tiled=True),
        preferred_element_type=jnp.float32,
    )
    sending = expert_out.astype(jnp.bfloat16).reshape(experts, capacity, weight_out.shape[2])
    returned = lax.all_to_all(sending, "expert", split_axis=0, concat_axis=0, tiled=True)
    mixed = jnp.dot(
        combine_weight,
        returned.reshape(experts * capacity, weight_out.shape[2]),
        preferred_element_type=jnp.float32,
    )
    return mixed.astype(jnp.bfloat16)


def solution(mesh):
    return jax.shard_map(
        per_device,
        mesh=mesh,
        in_specs=(
            P(("dp", "expert"), "tensor"),
            P(("dp", "expert"), None),
            P(("dp", "expert"), None),
            P("expert", None, "tensor", "dp"),
            P("expert", "dp", "tensor"),
        ),
        out_specs=P(("dp", "expert"), "tensor"),
        check_vma=False,
    )
```

profile of v0, /device:TPU:0, one launch (start us, length us, event | category | flops | bytes accessed | tf_op | source)
XLA Modules:
  0.0 244.5 jit_solution(11156711289392601985)
XLA Ops:
  6.5 0.8 copy.44
  7.6 1.2 reduce-window.6
  9.5 0.7 multiply_add_fusion
  10.2 0.7 convert_element_type.41
  10.8 1.2 fusion.8
  12.0 8.4 %psum.7 = f32[128,1]{0,1:T(1,128)S(1)} all-reduce(f32[128,1]{0,1:T(1,128)S(1)} %bitcast.52), channel_id=1, replica_groups=mesh['dp'=2,'expert'=4,'tensor'=4] {'tensor'}, use_global_device_ids=true, to_apply=%region_6.7 | all-reduce | flops 128 | bytes 1024 | tf_op jit(solution)/shard_map/psum | solution.py:13
  20.4 0.1 select_reduce_fusion
  20.6 1.6 convolution_convert_fusion
  22.2 36.3 %all_to_all.28 = bf16[4,96,1792]{2,1,0:T(8,128)(2,1)} all-to-all(bf16[4,96,1792]{2,1,0:T(8,128)(2,1)S(1)} %bitcast.47), channel_id=1, replica_groups=mesh['dp'=2,'expert'=4,'tensor'=4] {'expert'}, dimensions={0} | all-to-all | bytes 2752512 | tf_op jit(solution)/shard_map/all_to_all | solution.py:32
  58.6 39.7 %all-gather.5.cloned.1.call-done = bf16[768,1792]{1,0:T(8,128)(2,1)} async-done(((bf16[384,1792]{1,0:T(8,128)(2,1)}), bf16[768,1792]{1,0:T(8,128)(2,1)}) %all-gather.5.cloned.1.call-update) | async-done | bytes 2752528 | tf_op jit(solution)/shard_map/all_gather | solution.py:37
  98.3 7.6 %fusion.2 = f32[768,2,512]{2,0,1:T(8,128)} fusion(bf16[1,2,1792,512]{3,2,1,0:T(8,128)(2,1)} %param.8, bf16[768,1792]{1,0:T(8,128)(2,1)} %all-gather.5.cloned.1.call-done), kind=kOutput, calls=%fused_computation.2 | convolution fusion | flops 2818572288 | bytes 9568256 | tf_op jit(solution)/shard_map/rd,gdf->rgf/dot_general | solution.py:35
  105.9 0.7 all-gather.7.cloned.1.call-update
  106.6 37.1 %reduce-scatter.2.cloned.1.call-done = f32[768,2,128]{2,0,1:T(8,128)} async-done(((f32[768,2,512]{2,0,1:T(8,128)}), f32[768,2,128]{2,0,1:T(8,128)}) %reduce-scatter.2.cloned.1.call-update) | async-done | bytes 786448 | tf_op jit(solution)/shard_map/reduce_scatter | solution.py:41
  143.7 1.2 fusion.12
  145.0 0.5 broadcast.38
  145.5 0.8 reduce
  146.3 7.4 %all_to_all.29 = bf16[2,2,24576]{2,1,0:T(2,128)(2,1)S(1)} all-to-all(bf16[2,2,24576]{2,1,0:T(2,128)(2,1)S(1)} %reshape.61), channel_id=1, replica_groups=mesh['dp'=2,'expert'=4,'tensor'=4] {'dp'}, dimensions={0} | all-to-all | bytes 393216 | tf_op jit(solution)/shard_map/all_to_all | solution.py:43
  153.7 0.2 reshape.62
  153.9 7.7 %all-gather = bf16[384,2,1,512]{3,0,1,2:T(8,128)(2,1)S(1)} all-gather(bf16[384,2,1,128]{3,0,1,2:T(8,128)(2,1)S(1)} %bitcast.50), channel_id=2, replica_groups=mesh['dp'=2,'expert'=4,'tensor'=4] {'tensor'}, dimensions={3}, use_global_device_ids=true | all-gather | bytes 983040 | tf_op jit(solution)/shard_map/all_gather | solution.py:45
  161.6 0.4 copy.50
  162.0 34.2 %all-gather.7.cloned.1.call-done = bf16[1,1024,1792]{2,1,0:T(8,128)(2,1)} async-done(((bf16[1,512,1792]{2,1,0:T(8,128)(2,1)}), bf16[1,1024,1792]{2,1,0:T(8,128)(2,1)}) %all-gather.7.cloned.1.call-update) | async-done | bytes 3670032 | tf_op jit(solution)/shard_map/all_gather | solution.py:48
  196.1 3.7 %fusion.4 = bf16[384,1792]{1,0:T(8,128)(2,1)S(1)} fusion(bf16[384,1024]{0,1:T(8,128)(2,1)S(1)} %bitcast.49, bf16[1,1024,1792]{2,1,0:T(8,128)(2,1)} %all-gather.7.cloned.1.call-done), kind=kOutput, calls=%fused_computation.5 | convolution fusion | flops 1409974272 | bytes 5832704 | tf_op jit(solution)/shard_map/dot_general | solution.py:46
  199.8 37.0 %all_to_all.30 = bf16[4,96,1792]{2,1,0:T(8,128)(2,1)S(1)} all-to-all(bf16[4,96,1792]{2,1,0:T(8,128)(2,1)S(1)} %bitcast.48), channel_id=1, replica_groups=mesh['dp'=2,'expert'=4,'tensor'=4] {'expert'}, dimensions={0} | all-to-all | bytes 2752512 | tf_op jit(solution)/shard_map/all_to_all | solution.py:52
  236.8 1.2 convolution_convert_fusion.1
  (20 shorter events, 1.1 us)
Async XLA Ops:
  6.5 91.7 %all-gather.5.cloned.1.call-start = ((), (), s32[]{:S(2)}) async-start(), calls=%async_computation.4 | async-start | bytes 4128768 | tf_op jit(solution)/shard_map/all_gather | solution.py:37
  58.5 85.2 %reduce-scatter.2.cloned.1.call-start = ((), (), s32[]{:S(2)}) async-start(), calls=%async_computation.5 | async-start | bytes 3932160 | tf_op jit(solution)/shard_map/reduce_scatter | solution.py:41
  105.9 90.3 %all-gather.7.cloned.1.call-start = ((), (), s32[]{:S(2)}) async-start(), calls=%async_computation.6 | async-start | bytes 5505024 | tf_op jit(solution)/shard_map/all_gather | solution.py:48
Sparse Core Ops, SparseCore 0:
  58.6 39.6 all-gather.4
  106.0 37.7 reduce-scatter.1
  145.3 50.8 all-gather.6
where the time goes:
time: 245 us; the launch traced here: 244 us
  waiting for transfers between devices  112 us (46%)
  blocking collectives  96.8 us (40%)
  matrix products  14 us (6%)
  between operations  13.2 us (5%)
  other arithmetic  6.05 us (2%)
  local copies, waits for them, and re-layouts  2.69 us (1%)
    all_gather x1, waiting for transfers between devices, per_device(): lax.all_gather(slot_rows, 'dp', axis=0, tiled=True)  39.7 us
    reduce_scatter x1, waiting for transfers between devices, per_device(): lax.psum_scatter(partial_sums, 'tensor', scatter_dimension=2, tiled=True)  37.1 us
    all_to_all x1, blocking collectives, per_device(): lax.all_to_all(sending, 'expert', split_axis=0, concat_axis=0, tiled=True)  37 us
    all_to_all x1, blocking collectives, per_device(): lax.all_to_all(outgoing, 'expert', split_axis=0, concat_axis=0, tiled=True)  36.3 us
    all_gather x1, waiting for transfers between devices, per_device(): lax.all_gather(weight_out[0], 'dp', axis=0, tiled=True)  34.2 us
    psum x1, blocking collectives, per_device(): lax.psum(jnp.sum(wide * wide, axis=1, keepdims=True), 'tensor')  8.39 us
    all_gather x1, blocking collectives, per_device(): lax.all_gather(hidden, 'tensor', axis=2, tiled=True).reshape(row_count, -1)  7.73 us
    dot_general x1, matrix products, per_device(): jnp.einsum('rd,gdf->rgf', lax.all_gather(slot_rows, 'dp', axis=0, tiled=T...  7.55 us
  transfers between devices with their start and end apart: 3, of which 3 were waited for; matrix products, arithmetic and copies ran while one was open for 1% of the time, Pallas kernels for 0%

commit v1 on v0

v1 whole, which is shorter than its diff:
```python
import functools

import jax
import jax.numpy as jnp
from jax import lax
from jax.experimental import pallas as pl
from jax.experimental.pallas import tpu as pltpu
from jax.sharding import PartitionSpec as P

MESH = pl.DeviceIdType.MESH
F32 = jnp.float32
BF16 = jnp.bfloat16


def dot(a, b):
    return jnp.dot(a, b, preferred_element_type=F32)


def kernel(
    sizes,
    tokens,
    ids,
    ids_t,
    scores,
    w_in_hbm,
    w_out_hbm,
    mixed,
    w_in,
    w_out,
    slot_t,
    combine,
    outgoing,
    rows_in,
    part,
    part_in,
    hidden,
    down,
    down_in,
    home,
    home_in,
    w_sem,
    sz,
    rz,
    sx,
    rx,
    sp,
    rp,
    sh,
    rh,
    so,
    ro,
    sr,
    rr,
):
    n_dp, n_ex, n_t, cap = sizes
    d, e, t = lax.axis_index("dp"), lax.axis_index("expert"), lax.axis_index("tensor")
    group = n_ex // n_t
    ec = e // group
    tok, width = tokens.shape
    top = ids.shape[1]
    units = w_out.shape[0]
    width_all = width * n_t
    chunk_rows = group * cap

    def at(index, step, count):
        return lax.rem(index + step + count, count)

    def copy(src, dst, send, recv, axis, index):
        return pltpu.make_async_remote_copy(
            src_ref=src, dst_ref=dst, send_sem=send, recv_sem=recv,
            device_id={axis: index}, device_id_type=MESH,
        )

    barrier = pltpu.get_barrier_semaphore()
    for axis, me, count in (("dp", d, n_dp), ("expert", e, n_ex), ("tensor", t, n_t)):
        for step in range(1, count):
            pl.semaphore_signal(
                barrier, inc=1, device_id={axis: at(me, step, count)}, device_id_type=MESH
            )
    load_in = pltpu.make_async_copy(w_in_hbm.at[0], w_in, w_sem.at[0])
    load_out = pltpu.make_async_copy(w_out_hbm.at[0], w_out, w_sem.at[1])
    load_in.start()
    load_out.start()

    wide_ex = max(128, n_ex)
    ex_rows = lax.broadcasted_iota(jnp.int32, (wide_ex, tok), 0)
    named_t = ex_rows == ids_t[0:1, :]
    for k in range(1, top):
        named_t = named_t | (ex_rows == ids_t[k : k + 1, :])
    before = lax.broadcasted_iota(jnp.int32, (tok, tok), 0) < lax.broadcasted_iota(
        jnp.int32, (tok, tok), 1
    )
    count_t = dot(named_t.astype(F32).astype(BF16), before.astype(F32).astype(BF16))
    slot_t[...] = jnp.where(named_t, count_t, -1.0)
    slot_rows = lax.broadcasted_iota(jnp.int32, (cap, tok), 0).astype(F32)

    def picked(expert):
        pick = (slot_rows == slot_t[pl.ds(expert, 1), :]).astype(F32).astype(BF16)
        return dot(pick, tokens[...]).astype(BF16)

    def block(ref, lead, expert):
        if group == 1:
            return ref.at[lead, expert]
        return ref.at[lead, expert // group, pl.ds(pl.multiple_of(lax.rem(expert, group) * cap, cap), cap)]

    def send_z(expert):
        return copy(outgoing.at[expert], block(rows_in, 0, e), sz.at[expert], rz.at[e], "expert", expert)

    def wait_z(source):
        return copy(outgoing.at[source], block(rows_in, 0, source), sz.at[source], rz.at[source], "expert", source)

    pl.semaphore_wait(barrier, n_dp + n_ex + n_t - 3)

    outgoing[e] = picked(e)
    own = pltpu.make_async_copy(outgoing.at[e], block(rows_in, 0, e), w_sem.at[2])
    own.start()

    def forward_x(expert, step):
        return copy(
            block(rows_in, 0, expert), block(rows_in, n_dp - step, expert),
            sx.at[step, expert], rx.at[n_dp - step, expert], "dp", at(d, step, n_dp),
        )

    def wait_x(expert, h):
        return copy(
            block(rows_in, 0, expert), block(rows_in, h, expert),
            sx.at[h, expert], rx.at[h, expert], "dp", at(d, h, n_dp),
        )

    @pl.loop(1, n_ex)
    def _(step):
        expert = at(e, step, n_ex)
        outgoing[expert] = picked(expert)
        send_z(expert).start()

    own.wait()

    ex_lanes = lax.broadcasted_iota(jnp.int32, (tok, wide_ex), 1)
    named = ex_lanes == ids[:, 0:1]
    for k in range(1, top):
        named = named | (ex_lanes == ids[:, k : k + 1])
    after = lax.broadcasted_iota(jnp.int32, (tok, tok), 1) < lax.broadcasted_iota(
        jnp.int32, (tok, tok), 0
    )
    counts = dot(after.astype(F32).astype(BF16), named.astype(F32).astype(BF16))
    lanes = lax.broadcasted_iota(jnp.int32, (tok, n_ex * cap), 1).astype(F32)
    weights = jnp.zeros((tok, n_ex * cap), F32)
    for k in range(top):
        this = ids[:, k : k + 1]
        slot = jnp.sum(jnp.where(ex_lanes == this, counts, 0.0), axis=1, keepdims=True)
        target = this.astype(F32) * cap + slot
        weights = weights + jnp.where(lanes == target, scores[:, k : k + 1].astype(F32), 0.0)
    combine[...] = weights.astype(BF16)

    load_in.wait()

    def part_copy(h, c):
        return copy(part.at[h, c], part_in.at[h, t], sp.at[h, c], rp.at[h, t], "tensor", c)

    def project(h, c):
        rows = rows_in[h, c]
        for g in range(2):
            part[h, c, :, g * units : (g + 1) * units] = dot(rows, w_in[g]).astype(BF16)
        wide = rows.astype(F32)
        squares = jnp.sum(wide * wide, axis=1, keepdims=True)
        high = squares.astype(BF16).astype(F32)
        lane = lax.broadcasted_iota(jnp.int32, (chunk_rows, 128), 1)
        part[h, c, :, 2 * units :] = jnp.where(lane < 64, high, squares - high).astype(BF16)

        @pl.when(c != t)
        def _():
            part_copy(h, c).start()

    @pl.loop(0, n_t + 1)
    def _(step):
        @pl.when(step < n_t)
        def _():
            c = at(ec, -step, n_t)
            for i in range(group):
                source = c * group + i

                @pl.when(source != e)
                def _():
                    wait_z(source).wait_recv()

                for hop in range(1, n_dp):
                    forward_x(source, hop).start()
            project(0, c)

        @pl.when(step > 0)
        def _():
            c = at(ec, 1 - step, n_t)
            for h in range(1, n_dp):
                for i in range(group):
                    wait_x(c * group + i, h).wait_recv()
                project(h, c)

    def hidden_copy(h, step):
        return copy(hidden.at[h, t], hidden.at[h, t], sh.at[h, step], rh.at[h, t], "tensor", at(t, step, n_t))

    for h in range(n_dp):
        total = part[h, t].astype(F32)
        for step in range(1, n_t):
            s = at(t, step, n_t)
            copy(part.at[h, s], part_in.at[h, s], sp.at[h, s], rp.at[h, s], "tensor", s).wait_recv()
            total = total + part_in[h, s].astype(F32)
        squares = total[:, 2 * units : 2 * units + 1] + total[:, 2 * units + 64 : 2 * units + 65]
        scale = lax.rsqrt(squares / width_all + 1e-06)
        gate = total[:, :units] * scale
        up = total[:, units : 2 * units] * scale
        hidden[h, t] = (gate / (1.0 + jnp.exp(-gate)) * up).astype(BF16)
        for step in range(1, n_t):
            hidden_copy(h, step).start()

    load_out.wait()

    def wait_hidden(h, q):
        @pl.when(q != t)
        def _():
            copy(hidden.at[h, q], hidden.at[h, q], sh.at[h, 0], rh.at[h, q], "tensor", q).wait_recv()

    def down_copy(h, q):
        return copy(down.at[h, q], down_in.at[n_dp - h, q], so.at[h, q], ro.at[n_dp - h, q], "dp", at(d, h, n_dp))

    @pl.loop(0, n_t)
    def _(step):
        q = at(ec, 1 + step, n_t)
        for h in range(1, n_dp):
            wait_hidden(h, q)
            down[h, q] = dot(hidden[h, q], w_out[...]).astype(BF16)
            down_copy(h, q).start()

    def home_copy(expert):
        return copy(block(home, 0, expert), home_in.at[e], sr.at[expert], rr.at[e], "expert", expert)

    @pl.loop(0, n_t)
    def _(step):
        q = at(ec, 1 + step, n_t)
        wait_hidden(0, q)
        total = dot(hidden[0, q], w_out[...])
        for h in range(1, n_dp):
            copy(down.at[h, q], down_in.at[h, q], so.at[h, q], ro.at[h, q], "dp", at(d, h, n_dp)).wait_recv()
            total = total + down_in[h, q].astype(F32)
        home[0, q] = total.astype(BF16)
        for i in range(group):
            expert = q * group + i

            @pl.when(expert != e)
            def _():
                home_copy(expert).start()

            @pl.when(expert == e)
            def _():
                home_in[expert] = home[0, q, i * cap : (i + 1) * cap, :]

    @pl.loop(1, n_ex)
    def _(step):
        source = at(e, step, n_ex)
        copy(block(home, 0, source), home_in.at[source], sr.at[source], rr.at[source], "expert", source).wait_recv()

    mixed[...] = dot(combine[...], home_in[...].reshape(n_ex * cap, width)).astype(BF16)

    @pl.loop(1, n_ex)
    def _(step):
        expert = at(e, step, n_ex)
        send_z(expert).wait_send()
        home_copy(expert).wait_send()

    @pl.loop(0, n_ex)
    def _(expert):
        for hop in range(1, n_dp):
            forward_x(expert, hop).wait_send()

    for h in range(n_dp):
        for step in range(1, n_t):
            part_copy(h, at(t, step, n_t)).wait_send()
            hidden_copy(h, step).wait_send()
    for h in range(1, n_dp):
        for q in range(n_t):
            down_copy(h, q).wait_send()


def per_device(sizes, tokens, expert_ids, gate_scores, weight_in, weight_out):
    n_dp, n_ex, n_t, cap = sizes
    tok, width = tokens.shape
    units = weight_out.shape[1]
    chunk = n_ex // n_t * cap
    dma = pltpu.SemaphoreType.DMA
    vmem = pl.BlockSpec(memory_space=pltpu.VMEM)
    return pl.pallas_call(
        functools.partial(kernel, sizes),
        out_shape=jax.ShapeDtypeStruct((tok, width), BF16),
        in_specs=[vmem] * 4 + [pl.BlockSpec(memory_space=pl.ANY)] * 2,
        out_specs=vmem,
        scratch_shapes=[
            pltpu.VMEM((2, width, units), BF16),
            pltpu.VMEM((units, width), BF16),
            pltpu.VMEM((max(128, n_ex), tok), F32),
            pltpu.VMEM((tok, n_ex * cap), BF16),
            pltpu.VMEM((n_ex, cap, width), BF16),
            pltpu.VMEM((n_dp, n_t, chunk, width), BF16),
            pltpu.VMEM((n_dp, n_t, chunk, 2 * units + 128), BF16),
            pltpu.VMEM((n_dp, n_t, chunk, 2 * units + 128), BF16),
            pltpu.VMEM((n_dp, n_t, chunk, units), BF16),
            pltpu.VMEM((n_dp, n_t, chunk, width), BF16),
            pltpu.VMEM((n_dp, n_t, chunk, width), BF16),
            pltpu.VMEM((1, n_t, chunk, width), BF16),
            pltpu.VMEM((n_ex, cap, width), BF16),
            dma((3,)),
            dma((n_ex,)),
            dma((n_ex,)),
            dma((n_dp, n_ex)),
            dma((n_dp, n_ex)),
            dma((n_dp, n_t)),
            dma((n_dp, n_t)),
            dma((n_dp, n_t)),
            dma((n_dp, n_t)),
            dma((n_dp, n_t)),
            dma((n_dp, n_t)),
            dma((n_ex,)),
            dma((n_ex,)),
        ],
        compiler_params=pltpu.CompilerParams(
            collective_id=0, has_side_effects=True, vmem_limit_bytes=60 * 1024 * 1024
        ),
    )(tokens, expert_ids, expert_ids.T, gate_scores, weight_in, weight_out)


def solution(mesh):
    n_dp, n_ex, n_t = mesh.shape["dp"], mesh.shape["expert"], mesh.shape["tensor"]

    def whole(tokens, expert_ids, gate_scores, weight_in, weight_out):
        tok = tokens.shape[0] // (n_dp * n_ex)
        slots = min(3 * tok * expert_ids.shape[1] // (2 * n_ex), tok)
        cap = -(-slots // 16) * 16
        return jax.shard_map(
            functools.partial(per_device, (n_dp, n_ex, n_t, cap)),
            mesh=mesh,
            in_specs=(
                P(("dp", "expert"), "tensor"),
                P(("dp", "expert"), None),
                P(("dp", "expert"), None),
                P("expert", None, "tensor", "dp"),
                P("expert", "dp", "tensor"),
            ),
            out_specs=P(("dp", "expert"), "tensor"),
            check_vma=False,
        )(tokens, expert_ids, gate_scores, weight_in, weight_out)

    return whole
```

time: 245 us -> 110 us (0.45)
  waiting for transfers between devices: 112 us -> 0 us
  Pallas kernels: 0 us -> 104 us
  blocking collectives: 96.8 us -> 0 us
  matrix products: 14 us -> 0 us
  between operations: 13.2 us -> 0.01 us
  other arithmetic: 6.05 us -> 0 us
    pallas_call x0 -> x1, Pallas kernels: none -> 104 us  [per_device(): pl.pallas_call(functools.partial(kernel, sizes), out_shape=jax.ShapeDtype...]
    all_to_all x3 -> x0, blocking collectives: 80.6 us -> none  [the longest x1 37 us: per_device(): lax.all_to_all(sending, 'expert', split_axis=0, concat_axis=0, tiled=True)]
    all_gather x2 -> x0, waiting for transfers between devices: 73.9 us -> none  [the longest x1 39.7 us: per_device(): lax.all_gather(slot_rows, 'dp', axis=0, tiled=True)]
    reduce_scatter x1 -> x0, waiting for transfers between devices: 37.1 us -> none  [per_device(): lax.psum_scatter(partial_sums, 'tensor', scatter_dimension=2, tiled=True)]
    dot_general x4 -> x0, matrix products: 14 us -> none  [the longest x1 7.55 us: per_device(): jnp.einsum('rd,gdf->rgf', lax.all_gather(slot_rows, 'dp', axis=0, tiled=T...]
    psum x1 -> x0, blocking collectives: 8.39 us -> none  [per_device(): lax.psum(jnp.sum(wide * wide, axis=1, keepdims=True), 'tensor')]
    all_gather x1 -> x0, blocking collectives: 7.73 us -> none  [per_device(): lax.all_gather(hidden, 'tensor', axis=2, tiled=True).reshape(row_count, -1)]
    unnamed x4 -> x3, local copies, waits for them, and re-layouts: 1.07 us -> 4.6 us
  transfers between devices with their start and end apart: 3 -> 0, of which waited for: 3 -> 0; matrix products, arithmetic and copies ran while one was open for 1% -> 0% of each run, Pallas kernels for 0% -> 0%
where the time goes in v1:
time: 110 us; the launch traced here: 108 us
  Pallas kernels  104 us (95%)
  local copies, waits for them, and re-layouts  4.6 us (4%)
    pallas_call x1, Pallas kernels, per_device(): pl.pallas_call(functools.partial(kernel, sizes), out_shape=jax.ShapeDtype...  104 us
    unnamed x3, local copies, waits for them, and re-layouts  4.6 us

profile of v1, /device:TPU:0, one launch (start us, length us, event | category | flops | bytes accessed | tf_op | source)
XLA Modules:
  0.0 108.3 jit_solution(12695053132949431412)
XLA Ops:
  0.0 1.4 %copy.7.scores = bf16[128,2]{1,0:T(8,128)(2,1)} copy(bf16[128,2]{0,1:T(2,128)(2,1)} %param.7) | data formatting | bytes 1024 | tf_op args[2]
  1.4 1.4 %copy.6.ids = s32[128,2]{1,0:T(8,128)} copy(s32[128,2]{0,1:T(2,128)} %param.6) | data formatting | bytes 2048 | tf_op args[1]
  2.8 103.7 %shard_map.55 = bf16[128,1792]{1,0:T(8,128)(2,1)} custom-call(bf16[128,1792]{1,0:T(8,128)(2,1)} %tokens.1, s32[128,2]{1,0:T(8,128)} %copy.6.ids, s32[2,128]{1,0:T(2,128)} %bitcast.1, bf16[128,2]{1,0:T(8,128)(2,1)} %copy.7.scores, bf16[1,2,1792,512]{3,2,1,0:T(8,128)(2,1)} %w_in_hbm.1, bf16[1,512,1792]{2,1,0:T(8,128)(2,1)} %w_out_hbm.1), custom_call_target="tpu_custom_call" | custom-call | tf_op jit(solution)/shard_map/pallas_call | solution.py:290
  106.5 1.8 %copy.9 = bf16[128,1792]{1,0:T(8,128)(2,1)} copy(bf16[128,1792]{1,0:T(8,128)(2,1)} %shard_map.55) | data formatting | bytes 917504

commit v2 on v1

v2 whole, which is shorter than its diff:
```python
import functools

import jax
import jax.numpy as jnp
from jax import lax
from jax.experimental import pallas as pl
from jax.experimental.pallas import tpu as pltpu
from jax.sharding import PartitionSpec as P

MESH = pl.DeviceIdType.MESH
F32 = jnp.float32
BF16 = jnp.bfloat16


def dot(a, b):
    return jnp.dot(a, b, preferred_element_type=F32)


def kernel(
    sizes,
    tokens,
    ids,
    scores,
    w_in_hbm,
    w_out_hbm,
    mixed,
    w_in,
    w_out,
    squares,
    normed,
    slot_t,
    combine,
    outgoing,
    rows_in,
    part,
    part_in,
    hidden,
    keep,
    down,
    down_in,
    home,
    home_in,
    w_sem,
    sq,
    rq,
    sz,
    rz,
    sx,
    rx,
    sp,
    rp,
    sh,
    rh,
    so,
    ro,
    sr,
    rr,
):
    n_dp, n_ex, n_t, cap = sizes
    d, e, t = lax.axis_index("dp"), lax.axis_index("expert"), lax.axis_index("tensor")
    group = n_ex // n_t
    ec = e // group
    tok, width = tokens.shape
    top = ids.shape[1]
    units = w_out.shape[0]
    sub = units // n_t
    width_all = width * n_t

    def at(index, step, count):
        return lax.rem(index + step + count, count)

    def copy(src, dst, send, recv, axis, index):
        return pltpu.make_async_remote_copy(
            src_ref=src, dst_ref=dst, send_sem=send, recv_sem=recv,
            device_id={axis: index}, device_id_type=MESH,
        )

    barrier = pltpu.get_barrier_semaphore()
    for axis, me, count in (("dp", d, n_dp), ("expert", e, n_ex), ("tensor", t, n_t)):
        for step in range(1, count):
            pl.semaphore_signal(
                barrier, inc=1, device_id={axis: at(me, step, count)}, device_id_type=MESH
            )
    load_in = pltpu.make_async_copy(w_in_hbm.at[0], w_in, w_sem.at[0])
    load_out = pltpu.make_async_copy(w_out_hbm.at[0], w_out, w_sem.at[1])
    load_in.start()
    load_out.start()

    tok_rows = lax.broadcasted_iota(jnp.int32, (tok, tok), 0)
    tok_lanes = lax.broadcasted_iota(jnp.int32, (tok, tok), 1)

    def as_row(column):
        return jnp.sum(jnp.where(tok_rows == tok_lanes, column, 0.0), axis=0, keepdims=True)

    def as_column(row):
        return jnp.sum(jnp.where(tok_rows == tok_lanes, row, 0.0), axis=1, keepdims=True)

    wide = tokens[...].astype(F32)
    squares[t] = jnp.broadcast_to(as_row(jnp.sum(wide * wide, axis=1, keepdims=True)), (8, tok))

    def square_copy(step):
        return copy(squares.at[t], squares.at[t], sq.at[step], rq.at[t], "tensor", at(t, step, n_t))

    pl.semaphore_wait(barrier, n_dp + n_ex + n_t - 3)
    for step in range(1, n_t):
        square_copy(step).start()

    wide_ex = max(128, n_ex)
    ex_rows = lax.broadcasted_iota(jnp.int32, (wide_ex, tok), 0).astype(F32)
    named_t = ex_rows < 0.0
    for k in range(top):
        named_t = named_t | (ex_rows == as_row(ids[:, k : k + 1].astype(F32)))
    count_t = dot(named_t.astype(F32).astype(BF16), (tok_rows < tok_lanes).astype(F32).astype(BF16))
    slot_t[...] = jnp.where(named_t, count_t, -1.0)
    slot_rows = lax.broadcasted_iota(jnp.int32, (cap, tok), 0).astype(F32)

    for step in range(1, n_t):
        s = at(t, step, n_t)
        copy(squares.at[s], squares.at[s], sq.at[step], rq.at[s], "tensor", s).wait_recv()
    total_row = squares[0, 0:1, :]
    for s in range(1, n_t):
        total_row = total_row + squares[s, 0:1, :]
    scale = as_column(lax.rsqrt(total_row / width_all + 1e-06))
    normed[...] = (tokens[...].astype(F32) * scale).astype(BF16)

    def picked(expert):
        pick = (slot_rows == slot_t[pl.ds(expert, 1), :]).astype(F32).astype(BF16)
        return dot(pick, normed[...]).astype(BF16)

    def block(ref, lead, expert):
        if group == 1:
            return ref.at[lead, expert]
        return ref.at[lead, expert // group, pl.ds(pl.multiple_of(lax.rem(expert, group) * cap, cap), cap)]

    def send_z(expert):
        return copy(outgoing.at[expert], block(rows_in, 0, e), sz.at[expert], rz.at[e], "expert", expert)

    def wait_z(source):
        return copy(outgoing.at[source], block(rows_in, 0, source), sz.at[source], rz.at[source], "expert", source)

    def forward_x(src, expert, hop):
        return copy(
            src, block(rows_in, n_dp - hop, expert),
            sx.at[hop, expert], rx.at[n_dp - hop, expert], "dp", at(d, hop, n_dp),
        )

    def wait_x(expert, h):
        return copy(
            block(rows_in, 0, expert), block(rows_in, h, expert),
            sx.at[h, expert], rx.at[h, expert], "dp", at(d, h, n_dp),
        )

    outgoing[e] = picked(e)
    own = pltpu.make_async_copy(outgoing.at[e], block(rows_in, 0, e), w_sem.at[2])
    own.start()
    for hop in range(1, n_dp):
        forward_x(outgoing.at[e], e, hop).start()

    @pl.loop(1, n_ex)
    def _(step):
        expert = at(e, step, n_ex)
        outgoing[expert] = picked(expert)
        send_z(expert).start()

    ex_lanes = lax.broadcasted_iota(jnp.int32, (tok, wide_ex), 1)
    named = ex_lanes == ids[:, 0:1]
    for k in range(1, top):
        named = named | (ex_lanes == ids[:, k : k + 1])
    counts = dot((tok_lanes < tok_rows).astype(F32).astype(BF16), named.astype(F32).astype(BF16))
    lanes = lax.broadcasted_iota(jnp.int32, (tok, n_ex * cap), 1).astype(F32)
    weights = jnp.zeros((tok, n_ex * cap), F32)
    for k in range(top):
        this = ids[:, k : k + 1]
        slot = jnp.sum(jnp.where(ex_lanes == this, counts, 0.0), axis=1, keepdims=True)
        target = this.astype(F32) * cap + slot
        weights = weights + jnp.where(lanes == target, scores[:, k : k + 1].astype(F32), 0.0)
    combine[...] = weights.astype(BF16)

    own.wait()
    load_in.wait()
    load_out.wait()

    def part_copy(h, c, step):
        to = at(t, step, n_t)
        return copy(part.at[h, c, to], part_in.at[h, c, t], sp.at[h, c, step], rp.at[h, c, t], "tensor", to)

    def hidden_copy(h, c, step):
        to = at(t, step, n_t)
        return copy(hidden.at[h, c, t], hidden.at[h, c, t], sh.at[h, c, step], rh.at[h, c, t], "tensor", to)

    def down_copy(h, c):
        return copy(down.at[h, c], down_in.at[n_dp - h, c], so.at[h, c], ro.at[n_dp - h, c], "dp", at(d, h, n_dp))

    def project(h, c):
        @pl.when(h == 0)
        def _():
            for i in range(group):
                source = c * group + i

                @pl.when(source != e)
                def _():
                    wait_z(source).wait_recv()
                    for hop in range(1, n_dp):
                        forward_x(block(rows_in, 0, source), source, hop).start()

        @pl.when(h > 0)
        def _():
            for i in range(group):
                wait_x(c * group + i, h).wait_recv()

        rows = rows_in[h, c]
        for g in range(2):
            sums = dot(rows, w_in[g]).astype(BF16)
            for to in range(n_t):
                part[h, c, to, :, g * sub : (g + 1) * sub] = sums[:, to * sub : (to + 1) * sub]
        for step in range(1, n_t):
            part_copy(h, c, step).start()

    def activate(h, c):
        total = part[h, c, t].astype(F32)
        for step in range(1, n_t):
            s = at(t, step, n_t)
            copy(part.at[h, c, s], part_in.at[h, c, s], sp.at[h, c, step], rp.at[h, c, s], "tensor", s).wait_recv()
            total = total + part_in[h, c, s].astype(F32)
        gate, up = total[:, :sub], total[:, sub:]
        hidden[h, c, t] = (gate / (1.0 + jnp.exp(-gate)) * up).astype(BF16)
        for step in range(1, n_t):
            hidden_copy(h, c, step).start()

    def expand(h, c):
        for step in range(1, n_t):
            s = at(t, step, n_t)
            copy(hidden.at[h, c, s], hidden.at[h, c, s], sh.at[h, c, step], rh.at[h, c, s], "tensor", s).wait_recv()
        full = jnp.concatenate([hidden[h, c, s] for s in range(n_t)], axis=1)
        result = dot(full, w_out[...])

        @pl.when(h == 0)
        def _():
            keep[c] = result

        @pl.when(h > 0)
        def _():
            down[h, c] = result.astype(BF16)

            @pl.when(c != ec)
            def _():
                down_copy(h, c).start()

    def item(number):
        return lax.rem(number, n_dp), at(ec, -(number // n_dp), n_t)

    items = n_dp * n_t

    @pl.loop(0, items + 2)
    def _(step):
        @pl.when(step < items)
        def _():
            project(*item(step))

        @pl.when((step > 0) & (step <= items))
        def _():
            activate(*item(step - 1))

        @pl.when(step > 1)
        def _():
            expand(*item(step - 2))

    for h in range(1, n_dp):
        down_copy(h, ec).start()

    def home_copy(expert):
        return copy(block(home, 0, expert), home_in.at[e], sr.at[expert], rr.at[e], "expert", expert)

    @pl.loop(0, n_t)
    def _(step):
        q = at(ec, -1 - step, n_t)
        total = keep[q]
        for h in range(1, n_dp):
            copy(down.at[h, q], down_in.at[h, q], so.at[h, q], ro.at[h, q], "dp", at(d, h, n_dp)).wait_recv()
            total = total + down_in[h, q].astype(F32)
        home[0, q] = total.astype(BF16)
        for i in range(group):
            expert = q * group + i

            @pl.when(expert != e)
            def _():
                home_copy(expert).start()

            @pl.when(expert == e)
            def _():
                home_in[expert] = home[0, q, i * cap : (i + 1) * cap, :]

    @pl.loop(1, n_ex)
    def _(step):
        source = at(e, step, n_ex)
        copy(block(home, 0, source), home_in.at[source], sr.at[source], rr.at[source], "expert", source).wait_recv()

    mixed[...] = dot(combine[...], home_in[...].reshape(n_ex * cap, width)).astype(BF16)

    @pl.loop(1, n_ex)
    def _(step):
        expert = at(e, step, n_ex)
        send_z(expert).wait_send()
        home_copy(expert).wait_send()

    @pl.loop(0, n_ex)
    def _(expert):
        for hop in range(1, n_dp):
            forward_x(block(rows_in, 0, expert), expert, hop).wait_send()

    for step in range(1, n_t):
        square_copy(step).wait_send()

    @pl.loop(0, n_t)
    def _(c):
        for h in range(n_dp):
            for step in range(1, n_t):
                part_copy(h, c, step).wait_send()
                hidden_copy(h, c, step).wait_send()
        for h in range(1, n_dp):
            down_copy(h, c).wait_send()


def per_device(sizes, tokens, expert_ids, gate_scores, weight_in, weight_out):
    n_dp, n_ex, n_t, cap = sizes
    tok, width = tokens.shape
    units = weight_out.shape[1]
    chunk = n_ex // n_t * cap
    dma = pltpu.SemaphoreType.DMA
    vmem = pl.BlockSpec(memory_space=pltpu.VMEM)
    return pl.pallas_call(
        functools.partial(kernel, sizes),
        out_shape=jax.ShapeDtypeStruct((tok, width), BF16),
        in_specs=[vmem] * 3 + [pl.BlockSpec(memory_space=pl.ANY)] * 2,
        out_specs=vmem,
        scratch_shapes=[
            pltpu.VMEM((2, width, units), BF16),
            pltpu.VMEM((units, width), BF16),
            pltpu.VMEM((n_t, 8, tok), F32),
            pltpu.VMEM((tok, width), BF16),
            pltpu.VMEM((max(128, n_ex), tok), F32),
            pltpu.VMEM((tok, n_ex * cap), BF16),
            pltpu.VMEM((n_ex, cap, width), BF16),
            pltpu.VMEM((n_dp, n_t, chunk, width), BF16),
            pltpu.VMEM((n_dp, n_t, n_t, chunk, 2 * units // n_t), BF16),
            pltpu.VMEM((n_dp, n_t, n_t, chunk, 2 * units // n_t), BF16),
            pltpu.VMEM((n_dp, n_t, n_t, chunk, units // n_t), BF16),
            pltpu.VMEM((n_t, chunk, width), F32),
            pltpu.VMEM((n_dp, n_t, chunk, width), BF16),
            pltpu.VMEM((n_dp, n_t, chunk, width), BF16),
            pltpu.VMEM((1, n_t, chunk, width), BF16),
            pltpu.VMEM((n_ex, cap, width), BF16),
            dma((3,)),
            dma((n_t,)),
            dma((n_t,)),
            dma((n_ex,)),
            dma((n_ex,)),
            dma((n_dp, n_ex)),
            dma((n_dp, n_ex)),
            dma((n_dp, n_t, n_t)),
            dma((n_dp, n_t, n_t)),
            dma((n_dp, n_t, n_t)),
            dma((n_dp, n_t, n_t)),
            dma((n_dp, n_t)),
            dma((n_dp, n_t)),
            dma((n_ex,)),
            dma((n_ex,)),
        ],
        compiler_params=pltpu.CompilerParams(
            collective_id=0, has_side_effects=True, vmem_limit_bytes=60 * 1024 * 1024
        ),
    )(tokens, expert_ids, gate_scores, weight_in, weight_out)


def solution(mesh):
    n_dp, n_ex, n_t = mesh.shape["dp"], mesh.shape["expert"], mesh.shape["tensor"]

    def whole(tokens, expert_ids, gate_scores, weight_in, weight_out):
        tok = tokens.shape[0] // (n_dp * n_ex)
        slots = min(3 * tok * expert_ids.shape[1] // (2 * n_ex), tok)
        cap = -(-slots // 16) * 16
        return jax.shard_map(
            functools.partial(per_device, (n_dp, n_ex, n_t, cap)),
            mesh=mesh,
            in_specs=(
                P(("dp", "expert"), "tensor"),
                P(("dp", "expert"), None),
                P(("dp", "expert"), None),
                P("expert", None, "tensor", "dp"),
                P("expert", "dp", "tensor"),
            ),
            out_specs=P(("dp", "expert"), "tensor"),
            check_vma=False,
        )(tokens, expert_ids, gate_scores, weight_in, weight_out)

    return whole
```

time: 110 us -> 108 us (0.982); the launches traced: 108 us -> 108 us
  no operation moved by 1% of the time
where the time goes in v2:
time: 108 us
  Pallas kernels  103 us (95%)
  local copies, waits for them, and re-layouts  4.6 us (4%)
    pallas_call x1, Pallas kernels, per_device(): pl.pallas_call(functools.partial(kernel, sizes), out_shape=jax.ShapeDtype...  103 us
    unnamed x3, local copies, waits for them, and re-layouts  4.6 us

profile of v2, /device:TPU:0, one launch (start us, length us, event | category | flops | bytes accessed | tf_op | source)
XLA Modules:
  0.0 107.6 jit_solution(7694833754650333874)
XLA Ops:
  0.0 1.4 %copy.7.scores = bf16[128,2]{1,0:T(8,128)(2,1)} copy(bf16[128,2]{0,1:T(2,128)(2,1)} %param.7) | data formatting | bytes 1024 | tf_op args[2]
  1.4 1.4 %copy.6.ids = s32[128,2]{1,0:T(8,128)} copy(s32[128,2]{0,1:T(2,128)} %param.6) | data formatting | bytes 2048 | tf_op args[1]
  2.8 103.0 %shard_map.55 = bf16[128,1792]{1,0:T(8,128)(2,1)} custom-call(bf16[128,1792]{1,0:T(8,128)(2,1)} %tokens.1, s32[128,2]{1,0:T(8,128)} %copy.6.ids, bf16[128,2]{1,0:T(8,128)(2,1)} %copy.7.scores, bf16[1,2,1792,512]{3,2,1,0:T(8,128)(2,1)} %w_in_hbm.1, bf16[1,512,1792]{2,1,0:T(8,128)(2,1)} %w_out_hbm.1), custom_call_target="tpu_custom_call" | custom-call | tf_op jit(solution)/shard_map/pallas_call | solution.py:331
  105.8 1.8 %copy.9 = bf16[128,1792]{1,0:T(8,128)(2,1)} copy(bf16[128,1792]{1,0:T(8,128)(2,1)} %shard_map.55) | data formatting | bytes 917504

commit v3 on v2

--- a/solution.py
+++ b/solution.py
@@ -246,33 +246,15 @@
             def _():
                 down_copy(h, c).start()
 
-    def item(number):
-        return lax.rem(number, n_dp), at(ec, -(number // n_dp), n_t)
-
-    items = n_dp * n_t
-
-    @pl.loop(0, items + 2)
-    def _(step):
-        @pl.when(step < items)
-        def _():
-            project(*item(step))
-
-        @pl.when((step > 0) & (step <= items))
-        def _():
-            activate(*item(step - 1))
-
-        @pl.when(step > 1)
-        def _():
-            expand(*item(step - 2))
-
-    for h in range(1, n_dp):
-        down_copy(h, ec).start()
+            @pl.when((c == at(ec, 1, n_t)) & (h == n_dp - 1))
+            def _():
+                for far in range(1, n_dp):
+                    down_copy(far, ec).start()
 
     def home_copy(expert):
         return copy(block(home, 0, expert), home_in.at[e], sr.at[expert], rr.at[e], "expert", expert)
 
-    @pl.loop(0, n_t)
-    def _(step):
+    def collect(step):
         q = at(ec, -1 - step, n_t)
         total = keep[q]
         for h in range(1, n_dp):
@@ -289,6 +271,33 @@
             @pl.when(expert == e)
             def _():
                 home_in[expert] = home[0, q, i * cap : (i + 1) * cap, :]
+
+    def item(number):
+        return lax.rem(number, n_dp), at(ec, -(number // n_dp), n_t)
+
+    items = n_dp * n_t
+
+    @pl.loop(0, items + 2 + 1)
+    def _(step):
+        @pl.when(step < items)
+        def _():
+            project(*item(step))
+
+        @pl.when((step > 0) & (step <= items))
+        def _():
+            activate(*item(step - 1))
+
+        @pl.when((step > 1) & (step < items + 2))
+        def _():
+            expand(*item(step - 2))
+
+        for k in range(1, n_t):
+
+            @pl.when(step == (k + 1) * n_dp + 2)
+            def _():
+                collect(k - 1)
+
+    collect(n_t - 1)
 
     @pl.loop(1, n_ex)
     def _(step):

time: 108 us -> 101 us (0.935)
  Pallas kernels: 103 us -> 96.6 us
    pallas_call x1, Pallas kernels: 103 us -> 96.6 us  [per_device(): pl.pallas_call(functools.partial(kernel, sizes), out_shape=jax.ShapeDtype...]
where the time goes in v3:
time: 101 us
  Pallas kernels  96.6 us (96%)
  local copies, waits for them, and re-layouts  4.6 us (5%)
    pallas_call x1, Pallas kernels, per_device(): pl.pallas_call(functools.partial(kernel, sizes), out_shape=jax.ShapeDtype...  96.6 us
    unnamed x3, local copies, waits for them, and re-layouts  4.6 us

profile of v3, /device:TPU:0, one launch (start us, length us, event | category | flops | bytes accessed | tf_op | source)
XLA Modules:
  0.0 101.2 jit_solution(9996795186560438425)
XLA Ops:
  0.0 1.4 %copy.7.scores = bf16[128,2]{1,0:T(8,128)(2,1)} copy(bf16[128,2]{0,1:T(2,128)(2,1)} %param.7) | data formatting | bytes 1024 | tf_op args[2]
  1.4 1.4 %copy.6.ids = s32[128,2]{1,0:T(8,128)} copy(s32[128,2]{0,1:T(2,128)} %param.6) | data formatting | bytes 2048 | tf_op args[1]
  2.8 96.6 %shard_map.55 = bf16[128,1792]{1,0:T(8,128)(2,1)} custom-call(bf16[128,1792]{1,0:T(8,128)(2,1)} %tokens.1, s32[128,2]{1,0:T(8,128)} %copy.6.ids, bf16[128,2]{1,0:T(8,128)(2,1)} %copy.7.scores, bf16[1,2,1792,512]{3,2,1,0:T(8,128)(2,1)} %w_in_hbm.1, bf16[1,512,1792]{2,1,0:T(8,128)(2,1)} %w_out_hbm.1), custom_call_target="tpu_custom_call" | custom-call | tf_op jit(solution)/shard_map/pallas_call | solution.py:340
  99.4 1.8 %copy.9 = bf16[128,1792]{1,0:T(8,128)(2,1)} copy(bf16[128,1792]{1,0:T(8,128)(2,1)} %shard_map.55) | data formatting | bytes 917504
